TPU v7x, 32 devices: a whole 2x2x4 slice. The times are simulated.
32 devices in a mesh: rows: 16 (over z, y, x), cols: 2 (over core).
Axes of the slice: x: 2, y: 2, z: 4, core: 2. Of those that a mesh axis runs over, the one named last changes fastest.
Arguments:
- points: float32 [8, 4096], P(None, ('cols', 'rows')), may hold values from -6 to 6
- targets: float32 [4096], P(('cols', 'rows')), may hold values from -6 to 6
- noise: float32 [64, 4096], P(None, ('cols', 'rows')), may hold values from -6 to 6
- omega: float32 [8, 2048], P(None, 'rows'), may hold values from -12 to 12
- phase: float32 [2048], P('rows'), may hold values from -3.140625 to 3.140625
- weights: float32 [2048, 64], P('rows'), may hold values from -6 to 6
Outputs:
- posterior: float32 [64, 4096], P(None, ('cols', 'rows'))
- residual: float32 [64, 4096], P(None, ('cols', 'rows'))
All inputs are finite; a program needn't handle non-finite values.
Results may differ from a plain program's by a relative error of at most 0.02.
Values may be sent and summed in bfloat16 or wider, within the bound.
A program may use at most 64 MiB of HBM per device.

v0:
```python
import math
import jax
import jax.numpy as jnp
from jax import lax
from jax.sharding import PartitionSpec as P

ITERS = 2


def kernel_block(left, right):
    cross = lax.dot_general(
        left,
        right,
        (((0,), (0,)), ((), ())),
        precision=lax.Precision.HIGHEST,
        preferred_element_type=jnp.float32,
    )
    left_sq = jnp.sum(left * left, 0)
    right_sq = jnp.sum(right * right, 0)
    dist = left_sq[:, None] + right_sq[None, :] - 2.0 * cross
    return jnp.exp(-2.0 * dist).astype(jnp.bfloat16)


def body(points, targets, noise, omega, phase, weights):
    wide_omega, wide_phase, wide_weights = (
        lax.all_gather(omega, "rows", axis=1, tiled=True),
        lax.all_gather(phase, "rows", axis=0, tiled=True),
        lax.all_gather(weights, "rows", axis=0, tiled=True),
    )
    features = jnp.cos(
        lax.dot_general(
            wide_omega,
            points,
            (((0,), (0,)), ((), ())),
            precision=lax.Precision.HIGHEST,
            preferred_element_type=jnp.float32,
        )
        + wide_phase[:, None]
    )
    prior = math.sqrt(2.0 / wide_weights.shape[0]) * lax.dot_general(
        wide_weights,
        features,
        (((0,), (0,)), ((), ())),
        precision=lax.Precision.HIGHEST,
        preferred_element_type=jnp.float32,
    )
    rhs = targets[None, :] - prior - 0.5 * noise
    columns = lax.all_gather(points, ("rows", "cols"), axis=1, tiled=True)
    residual = rhs
    direction = rhs
    posterior = prior
    norm_now = lax.psum(jnp.sum(residual * residual, 1), ("rows", "cols"))
    for step in range(ITERS):
        low = direction.astype(jnp.bfloat16)
        kernel_part = jnp.dot(
            lax.all_gather(low, ("rows", "cols"), axis=1, tiled=True),
            kernel_block(columns, points),
            preferred_element_type=jnp.float32,
        )
        image = kernel_part + 0.25 * direction
        curve, mixed, square = lax.psum(
            (
                jnp.sum(direction * image, 1),
                jnp.sum(residual * image, 1),
                jnp.sum(image * image, 1),
            ),
            ("rows", "cols"),
        )
        alpha = norm_now / curve
        norm_next = norm_now - 2.0 * alpha * mixed + alpha * alpha * square
        posterior = posterior + alpha[:, None] * kernel_part
        residual = residual - alpha[:, None] * image
        if step + 1 < ITERS:
            direction = residual + (norm_next / norm_now)[:, None] * direction
            norm_now = norm_next
    return (posterior, residual)


def solution(mesh):
    return jax.shard_map(
        body,
        mesh=mesh,
        in_specs=(
            P(None, ("cols", "rows")),
            P(("cols", "rows")),
            P(None, ("cols", "rows")),
            P(None, "rows"),
            P("rows"),
            P("rows", None),
        ),
        out_specs=(P(None, ("cols", "rows")), P(None, ("cols", "rows"))),
        check_vma=False,
    )
```

profile of v0, /device:TPU:10, one launch (start us, length us, event | category | flops | bytes accessed | tf_op | source)
XLA Modules:
  0.0 325.9 jit_solution(18356954355384367689)
XLA Ops:
  0.6 0.0 copy-start.1
  0.6 0.0 copy-start.3
  0.7 0.0 copy-start.2
  0.7 30.7 %all_gather.18 = f32[8,2048]{1,0:T(8,128)S(1)} all-gather(f32[8,128]{1,0:T(8,128)} %param.9), channel_id=1, replica_groups=mesh['rows'=16,'cols'=2] {'rows'}, dimensions={1}, use_global_device_ids=true | all-gather | bytes 69632 | tf_op jit(solution)/shard_map/all_gather | solution.py:26
  31.3 40.7 %all-gather = f32[16,1,128]{2,1,0:T(1,128)S(1)} all-gather(f32[1,1,128]{2,1,0:T(1,128)} %bitcast.15), channel_id=1, replica_groups=mesh['rows'=16,'cols'=2] {'rows'}, dimensions={0}, use_global_device_ids=true | all-gather | bytes 8704 | tf_op jit(solution)/shard_map/all_gather | solution.py:27
  72.0 7.0 %fusion.4 = f32[2048,128]{1,0:T(8,128)S(1)} fusion(f32[8,2048]{1,0:T(8,128)S(1)} %all_gather.18, f32[8,128]{1,0:T(8,128)} %param.6, f32[2048]{0:T(1024)S(1)} %bitcast.14), kind=kOutput, calls=%fused_computation.6 | convolution fusion | flops 25427968 | bytes 1126400 | tf_op jit(solution)/shard_map/dot_general | solution.py:31
  79.1 0.0 copy-done.1
  79.1 0.0 copy-start
  79.1 38.9 %all_gather.20 = f32[2048,64]{0,1:T(8,128)S(1)} all-gather(f32[128,64]{0,1:T(8,128)S(1)} %copy-done.1), channel_id=1, replica_groups=mesh['rows'=16,'cols'=2] {'rows'}, dimensions={0}, use_global_device_ids=true | all-gather | bytes 557056 | tf_op jit(solution)/shard_map/all_gather | solution.py:28
  118.0 0.0 copy-done.3
  118.0 0.0 copy-done.2
  118.0 0.8 fusion.8
  118.8 0.0 copy-done
  118.8 38.3 %all_gather.22 = f32[8,4096]{1,0:T(8,128)S(1)} all-gather(f32[8,128]{1,0:T(8,128)S(1)} %copy-done), channel_id=1, replica_groups=mesh['rows'=16,'cols'=2] {'rows','cols'}, dimensions={1}, use_global_device_ids=true | all-gather | bytes 135168 | tf_op jit(solution)/shard_map/all_gather | solution.py:48
  157.1 3.9 %fusion.3 = bf16[4096,128]{1,0:T(8,128)(2,1)S(1)} fusion(f32[8,4096]{1,0:T(8,128)S(1)} %all_gather.22, f32[8,128]{1,0:T(8,128)S(1)} %copy-done, f32[128]{0:T(128)S(1)} %multiply_reduce_fusion.5, f32[4096]{0:T(1024)S(1)} %multiply_reduce_fusion), kind=kOutput, calls=%fused_computation.4 | convolution fusion | flops 52953088 | bytes 1200640 | tf_op jit(solution)/shard_map/dot_general | solution.py:11
  161.0 38.1 %all_gather.21 = bf16[64,4096]{1,0:T(8,128)(2,1)S(1)} all-gather(bf16[64,128]{1,0:T(8,128)(2,1)S(1)} %get-tuple-element.11), channel_id=1, replica_groups=mesh['rows'=16,'cols'=2] {'rows','cols'}, dimensions={1}, use_global_device_ids=true | all-gather | bytes 540672 | tf_op jit(solution)/shard_map/all_gather | solution.py:56
  199.1 0.4 multiply_reduce_fusion.3
  199.5 46.7 %all-reduce = (f32[64]{0:T(128)S(1)}, f32[64]{0:T(128)S(1)}, f32[64]{0:T(128)S(1)}) all-reduce(f32[64]{0:T(128)S(1)} %get-tuple-element.3, f32[64]{0:T(128)S(1)} %get-tuple-element.4, f32[64]{0:T(128)S(1)} %get-tuple-element.2), channel_id=1, replica_groups=mesh['rows'=16,'cols'=2] {'rows','cols'}, use_global_device_ids=true, to_apply=%region_7.0 | all-reduce | flops 192 | bytes 1536 | tf_op jit(solution)/shard_map/psum | solution.py:61
  246.2 0.1 fusion.6
  246.3 30.4 %all_gather.23 = bf16[64,4096]{1,0:T(8,128)(2,1)S(1)} all-gather(bf16[64,128]{1,0:T(8,128)(2,1)S(1)} %fusion.6), channel_id=1, replica_groups=mesh['rows'=16,'cols'=2] {'rows','cols'}, dimensions={1}, use_global_device_ids=true | all-gather | bytes 540672 | tf_op jit(solution)/shard_map/all_gather | solution.py:56
  276.7 0.4 multiply_reduce_fusion.1
  277.1 48.1 %psum.34 = f32[64]{0:T(128)S(1)} all-reduce(f32[64]{0:T(128)S(1)} %get-tuple-element.17), channel_id=1, replica_groups=mesh['rows'=16,'cols'=2] {'rows','cols'}, use_global_device_ids=true, to_apply=%region_9.0 | all-reduce | flops 64 | bytes 512 | tf_op jit(solution)/shard_map/psum | solution.py:61
  325.2 0.7 multiply_subtract_fusion
  (4 shorter events, 0.1 us)
Async XLA Ops:
  0.6 78.4 %copy-start.1 = (f32[128,64]{0,1:T(8,128)S(1)}, f32[128,64]{0,1:T(8,128)}, u32[]{:S(2)}) copy-start(f32[128,64]{0,1:T(8,128)} %param.11) | copy-start | bytes 98308
  0.6 117.4 %copy-start.3 = (f32[128]{0:T(128)S(1)}, f32[128]{0:T(128)}, u32[]{:S(2)}) copy-start(f32[128]{0:T(128)} %param.7) | copy-start | bytes 1540
  0.7 117.4 %copy-start.2 = (f32[64,128]{1,0:T(8,128)S(1)}, f32[64,128]{1,0:T(8,128)}, u32[]{:S(2)}) copy-start(f32[64,128]{1,0:T(8,128)} %param.8) | copy-start | bytes 98308
  79.1 39.7 %copy-start = (f32[8,128]{1,0:T(8,128)S(1)}, f32[8,128]{1,0:T(8,128)}, u32[]{:S(2)}) copy-start(f32[8,128]{1,0:T(8,128)} %param.6) | copy-start | bytes 12292
where the time goes:
time: 326 us
  blocking collectives  312 us (96%)
  matrix products  12.5 us (4%)
    psum x2, blocking collectives, body(): lax.psum((jnp.sum(direction * image, 1), jnp.sum(residual * image, 1), jn...  94.8 us
    all_gather x2, blocking collectives, body(): lax.all_gather(low, ('rows', 'cols'), axis=1, tiled=True)  68.4 us
    all_gather x1, blocking collectives, body(): lax.all_gather(phase, 'rows', axis=0, tiled=True)  40.7 us
    all_gather x1, blocking collectives, body(): lax.all_gather(weights, 'rows', axis=0, tiled=True)  38.9 us
    all_gather x1, blocking collectives, body(): columns = lax.all_gather(points, ('rows', 'cols'), axis=1, tiled=True)  38.3 us
    all_gather x1, blocking collectives, body(): lax.all_gather(omega, 'rows', axis=1, tiled=True)  30.7 us
    dot_general x1, matrix products, body(): lax.dot_general(wide_omega, points, (((0,), (0,)), ((), ())), precision=l...  7.01 us

commit v1 on v0

--- a/solution.py
+++ b/solution.py
@@ -3,6 +3,7 @@
 import jax.numpy as jnp
 from jax import lax
 from jax.sharding import PartitionSpec as P
+from jax.lax import psum
 
 ITERS = 2
 
@@ -58,13 +59,16 @@
             preferred_element_type=jnp.float32,
         )
         image = kernel_part + 0.25 * direction
-        curve, mixed, square = lax.psum(
-            (
-                jnp.sum(direction * image, 1),
-                jnp.sum(residual * image, 1),
-                jnp.sum(image * image, 1),
+        curve, mixed, square = psum(
+            psum(
+                (
+                    jnp.sum(direction * image, 1),
+                    jnp.sum(residual * image, 1),
+                    jnp.sum(image * image, 1),
+                ),
+                "cols",
             ),
-            ("rows", "cols"),
+            axis_name="rows",
         )
         alpha = norm_now / curve
         norm_next = norm_now - 2.0 * alpha * mixed + alpha * alpha * square

time: 326 us -> 369 us (1.13)
  the two profiles are of different devices: /device:TPU:10 before, /device:TPU:0 now
where the time goes in v1:
time: 369 us; the launch traced here: 368 us
  blocking collectives  354 us (96%)
  matrix products  12.5 us (3%)
    all_gather x2, blocking collectives, body(): lax.all_gather(low, ('rows', 'cols'), axis=1, tiled=True)  83 us
    psum x2, blocking collectives, body(): psum(psum((jnp.sum(direction * image, 1), jnp.sum(residual * image, 1), j...  73.1 us
    all_gather x1, blocking collectives, body(): lax.all_gather(omega, 'rows', axis=1, tiled=True)  43.1 us
    all_gather x1, blocking collectives, body(): lax.all_gather(weights, 'rows', axis=0, tiled=True)  40.4 us
    psum x1, blocking collectives, body(): norm_now = lax.psum(jnp.sum(residual * residual, 1), ('rows', 'cols'))  36.9 us
    all_gather x1, blocking collectives, body(): columns = lax.all_gather(points, ('rows', 'cols'), axis=1, tiled=True)  36.8 us
    all_gather x1, blocking collectives, body(): lax.all_gather(phase, 'rows', axis=0, tiled=True)  35.7 us

profile of v1, /device:TPU:0, one launch (start us, length us, event | category | flops | bytes accessed | tf_op | source)
XLA Modules:
  0.0 368.1 jit_solution(10869447307328696233)
XLA Ops:
  0.6 0.0 copy-start.1
  0.6 0.0 copy-start.3
  0.7 0.0 copy-start.2
  0.7 43.1 %all_gather.18 = f32[8,2048]{1,0:T(8,128)S(1)} all-gather(f32[8,128]{1,0:T(8,128)} %param.9), channel_id=1, replica_groups=mesh['rows'=16,'cols'=2] {'rows'}, dimensions={1}, use_global_device_ids=true | all-gather | bytes 69632 | tf_op jit(solution)/shard_map/all_gather | solution.py:27
  43.8 35.7 %all-gather = f32[16,1,128]{2,1,0:T(1,128)S(1)} all-gather(f32[1,1,128]{2,1,0:T(1,128)} %bitcast.15), channel_id=1, replica_groups=mesh['rows'=16,'cols'=2] {'rows'}, dimensions={0}, use_global_device_ids=true | all-gather | bytes 8704 | tf_op jit(solution)/shard_map/all_gather | solution.py:28
  79.5 7.0 %fusion.4 = f32[2048,128]{1,0:T(8,128)S(1)} fusion(f32[8,2048]{1,0:T(8,128)S(1)} %all_gather.18, f32[8,128]{1,0:T(8,128)} %param.6, f32[2048]{0:T(1024)S(1)} %bitcast.14), kind=kOutput, calls=%fused_computation.6 | convolution fusion | flops 25427968 | bytes 1126400 | tf_op jit(solution)/shard_map/dot_general | solution.py:32
  86.5 0.0 copy-done.1
  86.5 0.0 copy-start
  86.5 40.4 %all_gather.20 = f32[2048,64]{0,1:T(8,128)S(1)} all-gather(f32[128,64]{0,1:T(8,128)S(1)} %copy-done.1), channel_id=1, replica_groups=mesh['rows'=16,'cols'=2] {'rows'}, dimensions={0}, use_global_device_ids=true | all-gather | bytes 557056 | tf_op jit(solution)/shard_map/all_gather | solution.py:29
  127.0 0.0 copy-done.3
  127.0 0.0 copy-done.2
  127.0 0.8 fusion.8
  127.8 0.0 copy-done
  127.8 36.8 %all_gather.22 = f32[8,4096]{1,0:T(8,128)S(1)} all-gather(f32[8,128]{1,0:T(8,128)S(1)} %copy-done), channel_id=1, replica_groups=mesh['rows'=16,'cols'=2] {'rows','cols'}, dimensions={1}, use_global_device_ids=true | all-gather | bytes 135168 | tf_op jit(solution)/shard_map/all_gather | solution.py:49
  164.6 3.9 %fusion.3 = bf16[4096,128]{1,0:T(8,128)(2,1)S(1)} fusion(f32[8,4096]{1,0:T(8,128)S(1)} %all_gather.22, f32[8,128]{1,0:T(8,128)S(1)} %copy-done, f32[128]{0:T(128)S(1)} %multiply_reduce_fusion.5, f32[4096]{0:T(1024)S(1)} %multiply_reduce_fusion), kind=kOutput, calls=%fused_computation.4 | convolution fusion | flops 52953088 | bytes 1200640 | tf_op jit(solution)/shard_map/dot_general | solution.py:12
  168.5 39.8 %all_gather.21 = bf16[64,4096]{1,0:T(8,128)(2,1)S(1)} all-gather(bf16[64,128]{1,0:T(8,128)(2,1)S(1)} %get-tuple-element.12), channel_id=1, replica_groups=mesh['rows'=16,'cols'=2] {'rows','cols'}, dimensions={1}, use_global_device_ids=true | all-gather | bytes 540672 | tf_op jit(solution)/shard_map/all_gather | solution.py:57
  208.3 0.4 multiply_reduce_fusion.3
  208.8 2.5 all-reduce.1
  211.2 36.5 %all-reduce = (f32[64]{0:T(128)S(1)}, f32[64]{0:T(128)S(1)}) all-reduce(f32[64]{0:T(128)S(1)} %get-tuple-element.7, f32[64]{0:T(128)S(1)} %get-tuple-element.8), channel_id=1, replica_groups=mesh['rows'=16,'cols'=2] {'rows'}, use_global_device_ids=true, to_apply=%region_9.0 | all-reduce | flops 128 | bytes 1024 | tf_op jit(solution)/shard_map/psum | solution.py:62
  247.8 36.9 %psum.55 = f32[64]{0:T(128)S(1)} all-reduce(f32[64]{0:T(128)S(1)} %get-tuple-element.4), channel_id=1, replica_groups=mesh['rows'=16,'cols'=2] {'rows','cols'}, use_global_device_ids=true, to_apply=%region_1.0 | all-reduce | flops 64 | bytes 512 | tf_op jit(solution)/shard_map/psum | solution.py:53
  284.7 0.1 fusion.6
  284.8 43.2 %all_gather.23 = bf16[64,4096]{1,0:T(8,128)(2,1)S(1)} all-gather(bf16[64,128]{1,0:T(8,128)(2,1)S(1)} %fusion.6), channel_id=1, replica_groups=mesh['rows'=16,'cols'=2] {'rows','cols'}, dimensions={1}, use_global_device_ids=true | all-gather | bytes 540672 | tf_op jit(solution)/shard_map/all_gather | solution.py:57
  327.9 0.4 multiply_reduce_fusion.1
  328.3 2.5 psum.60
  330.8 36.5 %psum.61 = f32[64]{0:T(128)S(1)} all-reduce(f32[64]{0:T(128)S(1)} %psum.60), channel_id=1, replica_groups=mesh['rows'=16,'cols'=2] {'rows'}, use_global_device_ids=true, to_apply=%region_12.0 | all-reduce | flops 64 | bytes 512 | tf_op jit(solution)/shard_map/psum | solution.py:62
  367.4 0.7 multiply_subtract_fusion
  (4 shorter events, 0.1 us)
Async XLA Ops:
  0.6 85.9 %copy-start.1 = (f32[128,64]{0,1:T(8,128)S(1)}, f32[128,64]{0,1:T(8,128)}, u32[]{:S(2)}) copy-start(f32[128,64]{0,1:T(8,128)} %param.11) | copy-start | bytes 98308
  0.6 126.3 %copy-start.3 = (f32[128]{0:T(128)S(1)}, f32[128]{0:T(128)}, u32[]{:S(2)}) copy-start(f32[128]{0:T(128)} %param.7) | copy-start | bytes 1540
  0.7 126.3 %copy-start.2 = (f32[64,128]{1,0:T(8,128)S(1)}, f32[64,128]{1,0:T(8,128)}, u32[]{:S(2)}) copy-start(f32[64,128]{1,0:T(8,128)} %param.8) | copy-start | bytes 98308
  86.5 41.2 %copy-start = (f32[8,128]{1,0:T(8,128)S(1)}, f32[8,128]{1,0:T(8,128)}, u32[]{:S(2)}) copy-start(f32[8,128]{1,0:T(8,128)} %param.6) | copy-start | bytes 12292
